TPU v7x, 32 devices: a whole 2x2x4 slice. The times are simulated.
32 devices in a mesh: rows: 32 (over z, y, x, core).
Axes of the slice: x: 2, y: 2, z: 4, core: 2. Of those that a mesh axis runs over, the one named last changes fastest.
Arguments:
- tile_values: float32 [3584, 128, 128], P('rows'), as said below
- tile_row: int32 [3584], P('rows'), may hold values from 0 to 15, as said below
- tile_slot: int32 [3584], P('rows'), may hold values from 0 to 47, as said below
- tile_count: int32 [32], P('rows'), may hold values from 48 to 112, as said below
- requests: int32 [32, 32, 1], P('rows'), may hold values from 0 to 15
- right_side: float32 [512, 4, 128], P('rows')
Outputs:
- solution: float32 [512, 4, 128], P('rows')
- hessenberg: float32 [4, 4, 3], replicated
Inputs may be any that keep to these rules, and one draw needn't show every extreme that they name: `tile_row`: tile t < 16 of every device lies in block row t; it is the diagonal tile of that row. `tile_slot`: slot s < 16 is the device's own block s; slot 16 + o + q is the q-th block requested from device o; tile t < 48 of every device uses slot t. `tile_count`: some device uses all 112 slots. requests[d, o, q] is a block index among device o's 16 block rows. `tile_values`: tile t < 16 of every device holds the diagonal block of its row.
All inputs are finite; a program needn't handle non-finite values.
Results may differ from a plain program's by a relative error of at most 0.0003.
Values sent between devices are 32-bit elements; how exact they have to be, the bound alone decides.
A program may use at most 64 MiB of HBM per device.

v0:
```python
import jax
import jax.numpy as jnp
from jax import lax
from jax.sharding import PartitionSpec as P

ITERS = 3


epsilon = 1e-06
highest = lax.Precision.HIGHEST


def least_squares(hessenberg, beta_norm):
    krylov = hessenberg.shape[2]
    triangle = hessenberg
    target = jnp.zeros((hessenberg.shape[0], krylov + 1), jnp.float32).at[:, 0].set(beta_norm)
    cosines = []
    sine_list = []
    for column in range(krylov):
        column_vals = triangle[:, :, column]
        for earlier in range(column):
            first_entry = column_vals[:, earlier]
            second = column_vals[:, earlier + 1]
            column_vals = column_vals.at[:, earlier].set(
                cosines[earlier] * first_entry + sine_list[earlier] * second
            )
            column_vals = column_vals.at[:, earlier + 1].set(
                cosines[earlier] * second - sine_list[earlier] * first_entry
            )
        first_entry = column_vals[:, column]
        second = column_vals[:, column + 1]
        radius = jnp.sqrt(first_entry * first_entry + second * second)
        cosine = first_entry / radius
        sine_term = second / radius
        cosines.append(cosine)
        sine_list.append(sine_term)
        column_vals = column_vals.at[:, column].set(radius).at[:, column + 1].set(0.0)
        triangle = triangle.at[:, :, column].set(column_vals)
        leading = target[:, column]
        target = (
            target.at[:, column].set(cosine * leading).at[:, column + 1].set(-sine_term * leading)
        )
    weights = jnp.zeros((hessenberg.shape[0], krylov), jnp.float32)
    for column in reversed(range(krylov)):
        partial_sum = target[:, column] - jnp.sum(
            triangle[:, column, column + 1 : krylov] * weights[:, column + 1 :], axis=1
        )
        weights = weights.at[:, column].set(partial_sum / triangle[:, column, column])
    return weights


def local_squares(vector):
    return jnp.sum(vector * vector, axis=(0, 2))


def on_device(tile_values, tile_row, tile_slot, tile_count, requests, right_side):
    tile_total = tile_values.shape[0]
    row_blocks = right_side.shape[0]
    devices = lax.axis_size("rows")
    position = jnp.arange(tile_total, dtype=jnp.int32)
    live_mask = (position < tile_count[0]).astype(jnp.float32)
    block_ids = jnp.arange(row_blocks, dtype=jnp.int32)
    row_onehot = (tile_row[None, :] == block_ids[:, None]).astype(jnp.float32) * live_mask[None, :]
    own_requests = requests[0]
    asked_blocks = lax.all_to_all(
        own_requests, "rows", split_axis=0, concat_axis=0, tiled=True
    ).reshape(-1)
    beta_norm = jnp.sqrt(lax.psum(local_squares(right_side), "rows") + epsilon)
    basis_list = [right_side / beta_norm[None, :, None]]
    hessenberg = jnp.zeros((right_side.shape[1], ITERS + 1, ITERS), jnp.float32)
    for column in range(ITERS):
        vector = basis_list[column]
        outgoing = vector[asked_blocks].reshape(devices, -1, vector.shape[1], vector.shape[2])
        incoming = lax.all_to_all(outgoing, "rows", split_axis=0, concat_axis=0, tiled=True)
        slot_table = jnp.concatenate(
            [vector, incoming.reshape(-1, vector.shape[1], vector.shape[2])], axis=0
        )
        picked = slot_table[tile_slot]
        products = jnp.einsum("tij,tkj->tki", tile_values, picked, precision=highest)
        candidate = jnp.einsum("rt,tki->rki", row_onehot, products, precision=highest)
        stacked = jnp.stack(basis_list)
        local_terms = jnp.concatenate(
            [
                jnp.einsum("jrki,rki->jk", stacked, candidate, precision=highest),
                local_squares(candidate)[None, :],
            ],
            axis=0,
        )
        summed = lax.psum(local_terms, "rows")
        coefficients = summed[: column + 1]
        candidate = candidate - jnp.einsum("jk,jrki->rki", coefficients, stacked, precision=highest)
        hessenberg = hessenberg.at[:, : column + 1, column].set(jnp.transpose(coefficients))
        remainder = summed[column + 1] - jnp.sum(coefficients * coefficients, axis=0)
        length = jnp.sqrt(jnp.maximum(remainder, 0.0) + epsilon)
        hessenberg = hessenberg.at[:, column + 1, column].set(length)
        if column + 1 < ITERS:
            basis_list.append(candidate / length[None, :, None])
    weights = least_squares(hessenberg, beta_norm)
    solution = jnp.einsum("kj,jrki->rki", weights, jnp.stack(basis_list), precision=highest)
    return (solution, hessenberg)


def solution(mesh):
    return jax.shard_map(
        on_device,
        mesh=mesh,
        in_specs=(
            P("rows", None, None),
            P("rows"),
            P("rows"),
            P("rows"),
            P("rows", None, None),
            P("rows", None, None),
        ),
        out_specs=(P("rows", None, None), P()),
        check_vma=False,
    )
```

profile of v0, /device:TPU:0, one launch (start us, length us, event | category | flops | bytes accessed | tf_op | source)
XLA Modules:
  0.0 273.9 jit_solution(8367213065430252666)
XLA Ops:
  0.7 0.9 multiply_reduce_fusion.4
  1.6 1.3 copy.94
  2.9 7.3 %all-to-all-start = ((s32[32,1,1]{2,1,0:T(1,128)}), s32[32,1,1]{2,1,0:T(1,128)S(1)}, u32[]{:S(2)}, u32[]{:S(2)}) async-start(s32[32,1,1]{2,1,0:T(1,128)} %copy.94), calls=%async_computation | async-start | bytes 32768 | tf_op jit(solution)/shard_map/all_to_all | solution.py:65
  10.3 40.5 %psum.28 = f32[4]{0:T(128)S(1)} all-reduce(f32[4]{0:T(128)S(1)} %multiply_reduce_fusion.4), channel_id=1, replica_groups=mesh['rows'=32] {'rows'}, use_global_device_ids=true, to_apply=%region_1.0 | all-reduce | flops 4 | bytes 32 | tf_op jit(solution)/shard_map/psum | solution.py:68
  50.8 0.8 copy_divide_fusion
  51.6 0.8 fusion.69
  52.4 0.7 compare_select_fusion
  53.8 0.7 reduce.93
  54.5 1.2 gather_fusion
  55.7 4.5 %all-to-all-start.1 = ((f32[32,1,4,128]{3,2,1,0:T(4,128)}), f32[32,1,4,128]{3,2,1,0:T(4,128)S(1)}, u32[]{:S(2)}, u32[]{:S(2)}) async-start(f32[32,1,4,128]{3,2,1,0:T(4,128)} %bitcast.8), calls=%async_computation.1 | async-start | bytes 131072 | tf_op jit(solution)/shard_map/all_to_all | solution.py:74
  60.2 0.6 fusion.55
  60.8 6.8 %all-to-all-done.1 = f32[32,1,4,128]{3,2,1,0:T(4,128)S(1)} async-done(((f32[32,1,4,128]{3,2,1,0:T(4,128)}), f32[32,1,4,128]{3,2,1,0:T(4,128)S(1)}, u32[]{:S(2)}, u32[]{:S(2)}) %all-to-all-start.1) | async-done | bytes 65568 | tf_op jit(solution)/shard_map/all_to_all | solution.py:74
  67.6 0.7 gather_fusion.1
  68.3 13.6 %fusion.56 = f32[112,4,128]{2,1,0:T(4,128)S(1)} fusion(f32[112,4,128]{2,1,0:T(4,128)S(1)} %gather_fusion.1, f32[112,128,128]{2,1,0:T(8,128)} %param.68), kind=kOutput, calls=%fused_computation.141 | convolution fusion | flops 88080384 | bytes 7798784 | tf_op jit(solution)/shard_map/tij,tkj->tki/dot_general | solution.py:79
  82.0 0.3 multiply_reduce_fusion.3
  82.3 0.2 multiply_reduce_fusion
  82.5 38.3 %psum.29 = f32[2,4]{1,0:T(2,128)S(1)} all-reduce(f32[2,4]{1,0:T(2,128)S(1)} %pad_maximum_fusion.7), channel_id=1, replica_groups=mesh['rows'=32] {'rows'}, use_global_device_ids=true, to_apply=%region_3.0 | all-reduce | flops 8 | bytes 64 | tf_op jit(solution)/shard_map/psum | solution.py:89
  121.0 1.2 gather_fusion.2
  122.2 3.8 %all-to-all-start.2 = ((f32[32,1,4,128]{3,2,1,0:T(4,128)}), f32[32,1,4,128]{3,2,1,0:T(4,128)S(1)}, u32[]{:S(2)}, u32[]{:S(2)}) async-start(f32[32,1,4,128]{3,2,1,0:T(4,128)} %bitcast.16), calls=%async_computation.2 | async-start | bytes 131072 | tf_op jit(solution)/shard_map/all_to_all | solution.py:74
  126.0 0.6 fusion.54
  126.6 0.6 compare_reduce_fusion.3
  127.3 0.7 compare_reduce_fusion
  127.9 0.7 compare_reduce_fusion.1
  128.6 0.7 and_reduce_fusion
  129.4 3.9 %all-to-all-done.2 = f32[32,1,4,128]{3,2,1,0:T(4,128)S(1)} async-done(((f32[32,1,4,128]{3,2,1,0:T(4,128)}), f32[32,1,4,128]{3,2,1,0:T(4,128)S(1)}, u32[]{:S(2)}, u32[]{:S(2)}) %all-to-all-start.2) | async-done | bytes 65568 | tf_op jit(solution)/shard_map/all_to_all | solution.py:74
  133.3 0.7 gather_fusion.3
  134.0 13.6 %fusion.57 = f32[112,4,128]{2,1,0:T(4,128)S(1)} fusion(f32[112,4,128]{2,1,0:T(4,128)S(1)} %gather_fusion.3, f32[112,128,128]{2,1,0:T(8,128)} %param.68), kind=kOutput, calls=%fused_computation.142 | convolution fusion | flops 88080384 | bytes 7798784 | tf_op jit(solution)/shard_map/tij,tkj->tki/dot_general | solution.py:79
  147.7 0.3 multiply_reduce_fusion.2
  148.0 0.7 fusion.12
  148.8 38.3 %psum.30 = f32[3,4]{1,0:T(4,128)S(1)} all-reduce(f32[3,4]{1,0:T(4,128)S(1)} %pad_maximum_fusion.5), channel_id=1, replica_groups=mesh['rows'=32] {'rows'}, use_global_device_ids=true, to_apply=%region_5.0 | all-reduce | flops 12 | bytes 96 | tf_op jit(solution)/shard_map/psum | solution.py:89
  187.2 0.4 fusion.10
  187.7 1.2 gather_fusion.4
  188.9 3.7 %all-to-all-start.3 = ((f32[32,1,4,128]{3,2,1,0:T(4,128)}), f32[32,1,4,128]{3,2,1,0:T(4,128)S(1)}, u32[]{:S(2)}, u32[]{:S(2)}) async-start(f32[32,1,4,128]{3,2,1,0:T(4,128)} %bitcast.39), calls=%async_computation.3 | async-start | bytes 131072 | tf_op jit(solution)/shard_map/all_to_all | solution.py:74
  192.6 1.3 scatter.84
  194.0 6.1 %all-to-all-done.3 = f32[32,1,4,128]{3,2,1,0:T(4,128)S(1)} async-done(((f32[32,1,4,128]{3,2,1,0:T(4,128)}), f32[32,1,4,128]{3,2,1,0:T(4,128)S(1)}, u32[]{:S(2)}, u32[]{:S(2)}) %all-to-all-start.3) | async-done | bytes 65568 | tf_op jit(solution)/shard_map/all_to_all | solution.py:74
  200.1 0.7 gather_fusion.5
  200.8 13.6 %fusion.58 = f32[112,4,128]{2,1,0:T(4,128)S(1)} fusion(f32[112,4,128]{2,1,0:T(4,128)S(1)} %gather_fusion.5, f32[112,128,128]{2,1,0:T(8,128)} %param.68), kind=kOutput, calls=%fused_computation.143 | convolution fusion | flops 88080384 | bytes 7798784 | tf_op jit(solution)/shard_map/tij,tkj->tki/dot_general | solution.py:79
  214.4 0.3 multiply_reduce_fusion.1
  214.8 0.6 fusion.8
  215.5 38.5 %psum.31 = f32[4,4]{1,0:T(4,128)S(1)} all-reduce(f32[4,4]{1,0:T(4,128)S(1)} %pad_maximum_fusion.6), channel_id=1, replica_groups=mesh['rows'=32] {'rows'}, use_global_device_ids=true, to_apply=%region_11.0 | all-reduce | flops 16 | bytes 128 | tf_op jit(solution)/shard_map/psum | solution.py:89
  254.0 1.9 broadcast_select_fusion
  255.9 1.3 scatter.86
  257.3 0.7 copy.127
  258.2 0.7 fusion.33
  259.0 0.7 select_reduce_fusion.2
  260.0 0.7 add_select_fusion.2
  260.7 0.6 slice_select_fusion.3
  261.5 0.7 sqrt_select_fusion
  262.1 0.1 scatter.99
  262.3 0.8 select_reduce_fusion.1
  263.4 0.7 add_select_fusion.1
  264.1 0.7 slice_reduce_fusion.1
  264.8 0.1 scatter.105
  265.0 0.6 add_select_fusion
  265.6 0.1 scatter.106
  265.7 0.7 slice_select_fusion.1
  266.5 0.8 select_reduce_fusion
  267.5 1.2 fusion.36
  269.1 2.0 fusion.35
  271.3 0.2 multiply_reduce_fusion.5
  271.5 0.6 fusion.49
  272.2 0.6 slice_select_fusion
  272.9 0.4 fusion.6
  273.3 0.6 copy.175
  (82 shorter events, 2.9 us)
Async XLA Ops:
  0.6 81.7 %copy-start = (f32[16,4,128]{2,1,0:T(4,128)S(1)}, f32[16,4,128]{2,1,0:T(4,128)}, u32[]{:S(2)}) copy-start(f32[16,4,128]{2,1,0:T(4,128)} %param.73) | copy-start | bytes 98308
  0.6 81.3 %copy-start.1 = (s32[112]{0:T(128)S(1)}, s32[112]{0:T(128)}, u32[]{:S(2)}) copy-start(s32[112]{0:T(128)} %param.69) | copy-start | bytes 1348
  2.9 50.8 %all-to-all-start = ((s32[32,1,1]{2,1,0:T(1,128)}), s32[32,1,1]{2,1,0:T(1,128)S(1)}, u32[]{:S(2)}, u32[]{:S(2)}) async-start(s32[32,1,1]{2,1,0:T(1,128)} %copy.94), calls=%async_computation | async-start | bytes 32768 | tf_op jit(solution)/shard_map/all_to_all | solution.py:65
  55.7 11.9 %all-to-all-start.1 = ((f32[32,1,4,128]{3,2,1,0:T(4,128)}), f32[32,1,4,128]{3,2,1,0:T(4,128)S(1)}, u32[]{:S(2)}, u32[]{:S(2)}) async-start(f32[32,1,4,128]{3,2,1,0:T(4,128)} %bitcast.8), calls=%async_computation.1 | async-start | bytes 131072 | tf_op jit(solution)/shard_map/all_to_all | solution.py:74
  122.2 11.1 %all-to-all-start.2 = ((f32[32,1,4,128]{3,2,1,0:T(4,128)}), f32[32,1,4,128]{3,2,1,0:T(4,128)S(1)}, u32[]{:S(2)}, u32[]{:S(2)}) async-start(f32[32,1,4,128]{3,2,1,0:T(4,128)} %bitcast.16), calls=%async_computation.2 | async-start | bytes 131072 | tf_op jit(solution)/shard_map/all_to_all | solution.py:74
  188.9 11.1 %all-to-all-start.3 = ((f32[32,1,4,128]{3,2,1,0:T(4,128)}), f32[32,1,4,128]{3,2,1,0:T(4,128)S(1)}, u32[]{:S(2)}, u32[]{:S(2)}) async-start(f32[32,1,4,128]{3,2,1,0:T(4,128)} %bitcast.39), calls=%async_computation.3 | async-start | bytes 131072 | tf_op jit(solution)/shard_map/all_to_all | solution.py:74
where the time goes:
time: 275 us; the launch traced here: 274 us
  blocking collectives  156 us (57%)
  matrix products  43.9 us (16%)
  other arithmetic  21.6 us (8%)
  starting transfers between devices  19.3 us (7%)
  waiting for transfers between devices  16.7 us (6%)
  local copies, waits for them, and re-layouts  15.2 us (6%)
    psum x3, blocking collectives, on_device(): summed = lax.psum(local_terms, 'rows')  115 us
    dot_general x3, matrix products, on_device(): jnp.einsum('tij,tkj->tki', tile_values, picked, precision=highest)  40.9 us
    psum x1, blocking collectives, on_device(): beta_norm = jnp.sqrt(lax.psum(local_squares(right_side), 'rows') + epsilon)  40.5 us
    all_to_all x3, waiting for transfers between devices, on_device(): lax.all_to_all(outgoing, 'rows', split_axis=0, concat_axis=0, tiled=True)  16.7 us
    another operation x17, other arithmetic  13 us
    all_to_all x3, starting transfers between devices, on_device(): lax.all_to_all(outgoing, 'rows', split_axis=0, concat_axis=0, tiled=True)  12 us
    all_to_all x1, starting transfers between devices, on_device(): lax.all_to_all(own_requests, 'rows', split_axis=0, concat_axis=0, tiled=T...  7.33 us
  transfers between devices with their start and end apart: 4, of which 3 were waited for; matrix products, arithmetic and copies ran while one was open for 3% of the time, Pallas kernels for 0%

commit v1 on v0

v1 whole, which is shorter than its diff:
```python
import functools

import jax
import jax.numpy as jnp
from jax import lax
from jax.experimental import pallas as pl
from jax.experimental.pallas import tpu as pltpu
from jax.sharding import PartitionSpec as P

ITERS = 3
MESH = pl.DeviceIdType.MESH
epsilon = 1e-06
f32 = jnp.float32
bf16 = jnp.bfloat16


def split(x):
    high = x.astype(bf16).astype(f32)
    return high, x - high


def dot(a, b):
    return lax.dot_general(a, b, (((1,), (0,)), ((), ())), preferred_element_type=f32)


def dot_nt(a, b):
    return lax.dot_general(a, b, (((1,), (1,)), ((), ())), preferred_element_type=f32)


def twice(x):
    return jnp.concatenate([x, x], axis=0)


def kernel(
    n,
    chunk,
    unroll,
    tile_hbm,
    row_ref,
    count_ref,
    slot_ref,
    request_ref,
    right_ref,
    out_ref,
    hess_ref,
    tiles,
    parts,
    selector,
    spread,
    asked,
    outgoing,
    incoming,
    own,
    slots,
    table,
    products,
    tile_sem,
    ask_send,
    ask_recv,
    send_sem,
    recv_sem,
):
    me = lax.axis_index("rows")
    total, size, _ = tiles.shape
    blocks, systems, _ = right_ref.shape
    rows = 2 * systems
    chunks = total // chunk

    def tile_copy(index):
        where = pl.ds(index * chunk, chunk)
        return pltpu.make_async_copy(tile_hbm.at[where], tiles.at[where], tile_sem.at[index])

    for index in range(chunks):
        tile_copy(index).start()

    def peer_of(step):
        return lax.rem(me + step, n)

    def each_peer(body):
        def run(step, carry):
            body(step, peer_of(step))
            return carry

        lax.fori_loop(1, n, run, 0, unroll=min(unroll, n - 1))

    barrier = pltpu.get_barrier_semaphore()
    each_peer(
        lambda step, peer: pl.semaphore_signal(
            barrier, inc=1, device_id=(peer,), device_id_type=MESH
        )
    )

    lane = lax.broadcasted_iota(jnp.int32, (1, total), 1)
    live_row = jnp.where(lane < count_ref[0], row_ref[...], blocks)
    wide = total * rows
    from_tile = lax.broadcasted_iota(jnp.int32, (total, wide), 0)
    to_column = lax.broadcasted_iota(jnp.int32, (total, wide), 1)
    expand = jnp.where(to_column // rows == from_tile, 1.0, 0.0).astype(bf16)
    row_of = dot(jnp.broadcast_to(live_row.astype(f32), (8, total)).astype(bf16), expand)[0:1]
    for block in range(blocks):
        k_row = lax.broadcasted_iota(jnp.int32, (rows, wide), 0)
        q_col = lax.broadcasted_iota(jnp.int32, (rows, wide), 1)
        fits = (k_row % systems == q_col % systems) & (
            jnp.broadcast_to(row_of, (rows, wide)) == float(block)
        )
        spread[pl.ds(block * rows, rows), :] = jnp.where(fits, 1.0, 0.0)
    selector[...] = spread[...].astype(bf16)

    for block in range(blocks):
        own[0, block] = twice(right_ref[block])

    pl.semaphore_wait(barrier, n - 1)

    def ask_copy(step, peer):
        return pltpu.make_async_remote_copy(
            src_ref=request_ref,
            dst_ref=asked.at[me],
            send_sem=ask_send.at[step],
            recv_sem=ask_recv.at[me],
            device_id=(peer,),
            device_id_type=MESH,
        )

    def ask_arrival(peer):
        return pltpu.make_async_remote_copy(
            src_ref=request_ref,
            dst_ref=asked.at[peer],
            send_sem=ask_send.at[0],
            recv_sem=ask_recv.at[peer],
            device_id=(peer,),
            device_id_type=MESH,
        )

    each_peer(lambda step, peer: ask_copy(step, peer).start())

    def split_chunk(index, carry):
        tile_copy(index).wait()

        def split_tile(offset, carry):
            tile = index * chunk + offset
            high, low = split(tiles[tile])
            parts[tile, :, 0:size] = high.astype(bf16)
            parts[tile, :, size : 2 * size] = low.astype(bf16)
            return carry

        return lax.fori_loop(0, chunk, split_tile, carry, unroll=4)

    lax.fori_loop(0, chunks, split_chunk, 0)

    each_peer(lambda step, peer: ask_arrival(peer).wait_recv())
    each_peer(lambda step, peer: ask_copy(step, peer).wait_send())

    sub = lax.broadcasted_iota(jnp.int32, (rows, size), 0)
    lanes = lax.broadcasted_iota(jnp.int32, (rows, size), 1)
    system_of = sub % systems

    def message(parity, step, peer):
        return pltpu.make_async_remote_copy(
            src_ref=outgoing.at[parity, peer, pl.ds(0, systems + 1)],
            dst_ref=incoming.at[parity, me, pl.ds(0, systems + 1)],
            send_sem=send_sem.at[parity, peer],
            recv_sem=recv_sem.at[parity, me],
            device_id=(peer,),
            device_id_type=MESH,
        )

    def arrival(parity, peer):
        return pltpu.make_async_remote_copy(
            src_ref=outgoing.at[parity, peer, pl.ds(0, systems + 1)],
            dst_ref=incoming.at[parity, peer, pl.ds(0, systems + 1)],
            send_sem=send_sem.at[parity, peer],
            recv_sem=recv_sem.at[parity, peer],
            device_id=(peer,),
            device_id_type=MESH,
        )

    def exchange(parity, vector, sums):
        packed = jnp.zeros((rows, size), f32)
        for position, entry in enumerate(sums):
            packed = packed + jnp.where(lanes == rows * position + sub, entry, 0.0)
        packed = jnp.sum(packed[0:systems], axis=0, keepdims=True)
        incoming[parity, me, pl.ds(systems, 1), :] = packed

        def send(step, peer):
            outgoing[parity, peer, pl.ds(0, systems), :] = own[vector, asked[peer, 0, me]][0:systems]
            outgoing[parity, peer, pl.ds(systems, 1), :] = packed
            message(parity, step, peer).start()

        each_peer(send)

    def arrive(parity, count):
        each_peer(lambda step, peer: arrival(parity, peer).wait_recv())
        each_peer(lambda step, peer: message(parity, step, peer).wait_send())
        whole = jnp.sum(incoming[parity, :, systems, :], axis=0, keepdims=True)
        whole = jnp.broadcast_to(whole, (rows, size))
        return [
            jnp.broadcast_to(
                jnp.sum(
                    jnp.where(lanes == rows * position + system_of, whole, 0.0),
                    axis=1,
                    keepdims=True,
                ),
                (rows, size),
            )
            for position in range(count)
        ]

    def local_sum(x, y):
        return jnp.sum(jnp.sum(x * y, axis=0), axis=1, keepdims=True)

    def multiply():
        def step(group, carry):
            for offset in range(8):
                tile = group * 8 + offset
                x = table[slot_ref[tile]].astype(bf16)
                y = dot_nt(jnp.concatenate([x, x], axis=1), parts[tile])
                products[pl.ds(pl.multiple_of(tile * rows, rows), rows), :] = y
            return carry

        lax.fori_loop(0, total // 8, step, 0)
        high, low = split(products[...])
        result = dot(selector[...], high.astype(bf16)) + dot(selector[...], low.astype(bf16))
        return result.reshape(blocks, rows, size)

    def fill(index, scale, coefficients, parity):
        def place(slot, raw):
            for earlier, value in enumerate(coefficients):
                raw = raw - value * slots[earlier, slot]
            raw = raw * scale
            slots[index, slot] = raw
            high, low = split(raw)
            table[slot] = jnp.where(sub < systems, high, low)

        for block in range(blocks):
            place(block, own[index, block])

        def run(peer, carry):
            place(blocks + peer, twice(incoming[parity, peer, pl.ds(0, systems), :]))
            return carry

        lax.fori_loop(0, n, run, 0, unroll=min(8, n))

    def keep_own(parity, vector):
        incoming[parity, me, pl.ds(0, systems), :] = own[vector, request_ref[0, me]][0:systems]

    zero = jnp.zeros((rows, size), f32)
    right = own[0]
    exchange(0, 0, [local_sum(right, right)])
    keep_own(0, 0)
    (square,) = arrive(0, 1)
    beta = jnp.sqrt(square + epsilon)
    scale = 1.0 / beta
    gram = {(0, 0): square * scale * scale}
    coefficients = []
    triangle = []
    raw_columns = []
    rotations = []
    target = [beta]
    parity = 0
    for column in range(ITERS):
        fill(column, scale, coefficients, parity)
        candidate = multiply()
        parity = (column + 1) % 2
        sums = [local_sum(candidate, slots[i, 0:blocks]) for i in range(column + 1)]
        sums.append(local_sum(candidate, candidate))
        if column + 1 < ITERS:
            own[column + 1] = candidate
            exchange(parity, column + 1, sums)
            keep_own(parity, column + 1)
        else:
            own[ITERS] = candidate
            exchange(parity, column + 1, sums)
        if column >= 1:
            rotate(raw_columns[column - 1], rotations, triangle, target)
        summed = arrive(parity, column + 2)

        def inner(i, j):
            return gram[(min(i, j), max(i, j))]

        coefficients = []
        for i in range(column + 1):
            value = summed[i]
            for earlier in range(i):
                value = value - coefficients[earlier] * inner(earlier, i)
            coefficients.append(value)
        residual = summed[column + 1]
        for i in range(column + 1):
            residual = residual - 2.0 * coefficients[i] * summed[i]
        for i in range(column + 1):
            for j in range(column + 1):
                residual = residual + coefficients[i] * coefficients[j] * inner(i, j)
        residual = jnp.maximum(residual, 0.0)
        length = jnp.sqrt(residual + epsilon)
        scale = 1.0 / length
        if column + 1 < ITERS:
            for i in range(column + 1):
                value = summed[i]
                for earlier in range(column + 1):
                    value = value - coefficients[earlier] * inner(earlier, i)
                gram[(i, column + 1)] = value * scale
            gram[(column + 1, column + 1)] = residual * scale * scale
        raw_columns.append(coefficients + [length])
    rotate(raw_columns[ITERS - 1], rotations, triangle, target)
    weights = [None] * ITERS
    for column in reversed(range(ITERS)):
        value = target[column]
        for later in range(column + 1, ITERS):
            value = value - triangle[later][column] * weights[later]
        weights[column] = value / triangle[column][column]
    solved = weights[0] * slots[0, 0:blocks]
    for i in range(1, ITERS):
        solved = solved + weights[i] * slots[i, 0:blocks]
    for block in range(blocks):
        out_ref[block] = solved[block, 0:systems]
    for system in range(systems):
        picture = zero
        for column in range(ITERS):
            for i in range(column + 2):
                picture = jnp.where(
                    (sub == i) & (lanes == column),
                    jnp.broadcast_to(raw_columns[column][i][system : system + 1], (rows, size)),
                    picture,
                )
        hess_ref[system] = picture[0 : ITERS + 1, 0:ITERS]


def rotate(column, rotations, triangle, target):
    column = list(column)
    for i, (cosine, sine) in enumerate(rotations):
        first, second = column[i], column[i + 1]
        column[i] = cosine * first + sine * second
        column[i + 1] = cosine * second - sine * first
    last = len(column) - 2
    first, second = column[last], column[last + 1]
    radius = jnp.sqrt(first * first + second * second)
    cosine, sine = first / radius, second / radius
    rotations.append((cosine, sine))
    column[last] = radius
    triangle.append(column[: last + 1])
    leading = target[last]
    target[last] = cosine * leading
    target.append(-sine * leading)


def on_device(tile_values, tile_row, tile_slot, tile_count, requests, right_side):
    n = lax.axis_size("rows")
    total, size, _ = tile_values.shape
    blocks, systems, _ = right_side.shape
    rows = 2 * systems
    chunk = 16 if total % 16 == 0 else 1
    smem = pl.BlockSpec(memory_space=pltpu.SMEM)
    vmem = pl.BlockSpec(memory_space=pltpu.VMEM)
    dma = pltpu.SemaphoreType.DMA
    return pl.pallas_call(
        functools.partial(kernel, n, chunk, 8),
        out_shape=(
            jax.ShapeDtypeStruct((blocks, systems, size), f32),
            jax.ShapeDtypeStruct((systems, ITERS + 1, ITERS), f32),
        ),
        in_specs=[pl.BlockSpec(memory_space=pl.ANY), vmem, smem, smem, smem, vmem],
        out_specs=(vmem, vmem),
        scratch_shapes=[
            pltpu.VMEM((total, size, size), f32),
            pltpu.VMEM((total, size, 2 * size), bf16),
            pltpu.VMEM((blocks * rows, total * rows), bf16),
            pltpu.VMEM((blocks * rows, total * rows), f32),
            pltpu.SMEM((n, 1, n), jnp.int32),
            pltpu.VMEM((2, n, 8, size), f32),
            pltpu.VMEM((2, n, 8, size), f32),
            pltpu.VMEM((ITERS + 1, blocks, rows, size), f32),
            pltpu.VMEM((ITERS, blocks + n, rows, size), f32),
            pltpu.VMEM((blocks + n, rows, size), f32),
            pltpu.VMEM((total * rows, size), f32),
            dma((total // chunk,)),
            dma((n,)),
            dma((n,)),
            dma((2, n)),
            dma((2, n)),
        ],
        compiler_params=pltpu.CompilerParams(
            collective_id=0, has_side_effects=True, vmem_limit_bytes=60 * 1024 * 1024
        ),
        name="cycle",
    )(
        tile_values,
        tile_row.reshape(1, total),
        tile_count,
        tile_slot,
        requests.reshape(1, n),
        right_side,
    )


def solution(mesh):
    return jax.shard_map(
        on_device,
        mesh=mesh,
        in_specs=(
            P("rows", None, None),
            P("rows"),
            P("rows"),
            P("rows"),
            P("rows", None, None),
            P("rows", None, None),
        ),
        out_specs=(P("rows", None, None), P()),
        check_vma=False,
    )
```

time: 275 us -> 51 us (0.19)
  blocking collectives: 156 us -> 0 us
  Pallas kernels: 0 us -> 46.7 us
  matrix products: 43.9 us -> 0 us
  other arithmetic: 21.6 us -> 0 us
  starting transfers between devices: 19.3 us -> 0 us
  waiting for transfers between devices: 16.7 us -> 0 us
  local copies, waits for them, and re-layouts: 15.2 us -> 2.76 us
    psum x4 -> x0, blocking collectives: 156 us -> none  [the longest x3 115 us: on_device(): summed = lax.psum(local_terms, 'rows')]
    pallas_call x0 -> x1, Pallas kernels: none -> 46.7 us  [on_device(): pl.pallas_call(functools.partial(kernel, n, chunk, 8), out_shape=(jax.Sha...]
    dot_general x10 -> x0, matrix products: 43.9 us -> none  [the longest x3 40.9 us: on_device(): jnp.einsum('tij,tkj->tki', tile_values, picked, precision=highest)]
    all_to_all x4 -> x0, starting transfers between devices: 19.3 us -> none  [the longest x3 12 us: on_device(): lax.all_to_all(outgoing, 'rows', split_axis=0, concat_axis=0, tiled=True)]
    all_to_all x4 -> x0, waiting for transfers between devices: 16.7 us -> none  [the longest x3 16.7 us: on_device(): lax.all_to_all(outgoing, 'rows', split_axis=0, concat_axis=0, tiled=True)]
    another operation x20 -> x0, other arithmetic: 13.8 us -> none
    gather x6 -> x0, local copies, waits for them, and re-layouts: 5.85 us -> none  [the longest x3 3.66 us: on_device(): vector[asked_blocks].reshape(devices, -1, vector.shape[1], vector.shape[2])]
    scatter x24 -> x0, local copies, waits for them, and re-layouts: 3.69 us -> none  [the longest x3 2.62 us: on_device(): hessenberg.at[:, :column + 1, column].set(jnp.transpose(coefficients))]
  transfers between devices with their start and end apart: 4 -> 0, of which waited for: 3 -> 0; matrix products, arithmetic and copies ran while one was open for 3% -> 0% of each run, Pallas kernels for 0% -> 0%
where the time goes in v1:
time: 51 us; the launch traced here: 50.7 us
  Pallas kernels  46.7 us (92%)
  local copies, waits for them, and re-layouts  2.76 us (5%)
  between operations  1.29 us (3%)
    pallas_call x1, Pallas kernels, on_device(): pl.pallas_call(functools.partial(kernel, n, chunk, 8), out_shape=(jax.Sha...  46.7 us
    pallas_call x1, local copies, waits for them, and re-layouts, on_device(): pl.pallas_call(functools.partial(kernel, n, chunk, 8), out_shape=(jax.Sha...  1.39 us
    unnamed x1, local copies, waits for them, and re-layouts  1.37 us

profile of v1, /device:TPU:0, one launch (start us, length us, event | category | flops | bytes accessed | tf_op | source)
XLA Modules:
  0.0 50.7 jit_solution(4521178331012170605)
XLA Ops:
  1.3 46.7 %cycle.1 = (f32[16,4,128]{2,1,0:T(4,128)}, f32[4,4,3]{2,1,0:T(4,128)}) custom-call(f32[112,128,128]{2,1,0:T(8,128)} %tile_hbm.1, s32[1,112]{1,0:T(1,128)} %bitcast.2, s32[1]{0:T(128)S(6)} %copy.10.count_ref, s32[112]{0:T(128)} %slot_ref.1, s32[1,32]{1,0:T(1,128)} %bitcast.3, f32[16,4,128]{2,1,0:T(4,128)} %right_ref.1), custom_call_target="tpu_custom_call" | custom-call | tf_op jit(solution)/shard_map/cycle/pallas_call | solution.py:354
  47.9 1.4 %copy.8 = f32[4,4,3]{1,0,2:T(4,128)} copy(f32[4,4,3]{2,1,0:T(4,128)} %get-tuple-element.3) | data formatting | bytes 384 | tf_op jit(solution)/shard_map/cycle/pallas_call | solution.py:354
  49.3 1.4 %copy.11 = f32[16,4,128]{2,1,0:T(4,128)} copy(f32[16,4,128]{2,1,0:T(4,128)} %get-tuple-element.6) | data formatting | bytes 65536

commit v2 on v1

--- a/solution.py
+++ b/solution.py
@@ -21,10 +21,6 @@
 
 def dot(a, b):
     return lax.dot_general(a, b, (((1,), (0,)), ((), ())), preferred_element_type=f32)
-
-
-def dot_nt(a, b):
-    return lax.dot_general(a, b, (((1,), (1,)), ((), ())), preferred_element_type=f32)
 
 
 def twice(x):
@@ -65,6 +61,7 @@
     blocks, systems, _ = right_ref.shape
     rows = 2 * systems
     chunks = total // chunk
+    batch = max(b for b in range(1, 57) if total % b == 0)
 
     def tile_copy(index):
         where = pl.ds(index * chunk, chunk)
@@ -91,7 +88,7 @@
     )
 
     lane = lax.broadcasted_iota(jnp.int32, (1, total), 1)
-    live_row = jnp.where(lane < count_ref[0], row_ref[...], blocks)
+    live_row = jnp.where(lane < count_ref[...], row_ref[...], blocks)
     wide = total * rows
     from_tile = lax.broadcasted_iota(jnp.int32, (total, wide), 0)
     to_column = lax.broadcasted_iota(jnp.int32, (total, wide), 1)
@@ -138,9 +135,9 @@
 
         def split_tile(offset, carry):
             tile = index * chunk + offset
-            high, low = split(tiles[tile])
-            parts[tile, :, 0:size] = high.astype(bf16)
-            parts[tile, :, size : 2 * size] = low.astype(bf16)
+            high, low = split(tiles[tile].T)
+            parts[tile, 0:size, :] = high.astype(bf16)
+            parts[tile, size : 2 * size, :] = low.astype(bf16)
             return carry
 
         return lax.fori_loop(0, chunk, split_tile, carry, unroll=4)
@@ -210,14 +207,14 @@
 
     def multiply():
         def step(group, carry):
-            for offset in range(8):
-                tile = group * 8 + offset
+            for offset in range(batch):
+                tile = group * batch + offset
                 x = table[slot_ref[tile]].astype(bf16)
-                y = dot_nt(jnp.concatenate([x, x], axis=1), parts[tile])
+                y = dot(jnp.concatenate([x, x], axis=1), parts[tile])
                 products[pl.ds(pl.multiple_of(tile * rows, rows), rows), :] = y
             return carry
 
-        lax.fori_loop(0, total // 8, step, 0)
+        lax.fori_loop(0, total // batch, step, 0)
         high, low = split(products[...])
         result = dot(selector[...], high.astype(bf16)) + dot(selector[...], low.astype(bf16))
         return result.reshape(blocks, rows, size)
@@ -357,11 +354,11 @@
             jax.ShapeDtypeStruct((blocks, systems, size), f32),
             jax.ShapeDtypeStruct((systems, ITERS + 1, ITERS), f32),
         ),
-        in_specs=[pl.BlockSpec(memory_space=pl.ANY), vmem, smem, smem, smem, vmem],
+        in_specs=[pl.BlockSpec(memory_space=pl.ANY), vmem, vmem, smem, smem, vmem],
         out_specs=(vmem, vmem),
         scratch_shapes=[
             pltpu.VMEM((total, size, size), f32),
-            pltpu.VMEM((total, size, 2 * size), bf16),
+            pltpu.VMEM((total, 2 * size, size), bf16),
             pltpu.VMEM((blocks * rows, total * rows), bf16),
             pltpu.VMEM((blocks * rows, total * rows), f32),
             pltpu.SMEM((n, 1, n), jnp.int32),
@@ -384,7 +381,7 @@
     )(
         tile_values,
         tile_row.reshape(1, total),
-        tile_count,
+        tile_count.reshape(1, 1),
         tile_slot,
         requests.reshape(1, n),
         right_side,

time: 51 us -> 44.9 us (0.88)
  Pallas kernels: 46.7 us -> 40.5 us
    pallas_call x1, Pallas kernels: 46.7 us -> 40.5 us  [on_device(): pl.pallas_call(functools.partial(kernel, n, chunk, 8), out_shape=(jax.Sha...]
where the time goes in v2:
time: 44.9 us; the launch traced here: 44.6 us
  Pallas kernels  40.5 us (90%)
  local copies, waits for them, and re-layouts  2.76 us (6%)
  between operations  1.29 us (3%)
    pallas_call x1, Pallas kernels, on_device(): pl.pallas_call(functools.partial(kernel, n, chunk, 8), out_shape=(jax.Sha...  40.5 us
    pallas_call x1, local copies, waits for them, and re-layouts, on_device(): pl.pallas_call(functools.partial(kernel, n, chunk, 8), out_shape=(jax.Sha...  1.39 us
    unnamed x1, local copies, waits for them, and re-layouts  1.37 us

profile of v2, /device:TPU:0, one launch (start us, length us, event | category | flops | bytes accessed | tf_op | source)
XLA Modules:
  0.0 44.6 jit_solution(6979543218735867833)
XLA Ops:
  1.3 40.5 %cycle.1 = (f32[16,4,128]{2,1,0:T(4,128)}, f32[4,4,3]{2,1,0:T(4,128)}) custom-call(f32[112,128,128]{2,1,0:T(8,128)} %tile_hbm.1, s32[1,112]{1,0:T(1,128)} %bitcast.4, s32[1,1]{1,0:T(1,128)} %bitcast.3.count_ref, s32[112]{0:T(128)} %slot_ref.1, s32[1,32]{1,0:T(1,128)} %bitcast.5, f32[16,4,128]{2,1,0:T(4,128)} %right_ref.1), custom_call_target="tpu_custom_call" | custom-call | tf_op jit(solution)/shard_map/cycle/pallas_call | solution.py:351
  41.8 1.4 %copy.8 = f32[4,4,3]{1,0,2:T(4,128)} copy(f32[4,4,3]{2,1,0:T(4,128)} %get-tuple-element.3) | data formatting | bytes 384 | tf_op jit(solution)/shard_map/cycle/pallas_call | solution.py:351
  43.2 1.4 %copy.11 = f32[16,4,128]{2,1,0:T(4,128)} copy(f32[16,4,128]{2,1,0:T(4,128)} %get-tuple-element.6) | data formatting | bytes 65536

commit v3 on v2

--- a/solution.py
+++ b/solution.py
@@ -309,16 +309,11 @@
         solved = solved + weights[i] * slots[i, 0:blocks]
     for block in range(blocks):
         out_ref[block] = solved[block, 0:systems]
-    for system in range(systems):
+    for column in range(ITERS):
         picture = zero
-        for column in range(ITERS):
-            for i in range(column + 2):
-                picture = jnp.where(
-                    (sub == i) & (lanes == column),
-                    jnp.broadcast_to(raw_columns[column][i][system : system + 1], (rows, size)),
-                    picture,
-                )
-        hess_ref[system] = picture[0 : ITERS + 1, 0:ITERS]
+        for i in range(column + 2):
+            picture = jnp.where(lanes == i, raw_columns[column][i], picture)
+        hess_ref[column] = picture[0:systems, 0 : ITERS + 1]
 
 
 def rotate(column, rotations, triangle, target):
@@ -339,6 +334,11 @@
     target.append(-sine * leading)
 
 
+def hand_on(solved_ref, picture_ref, out_ref, hess_ref):
+    out_ref[...] = solved_ref[...]
+    hess_ref[...] = picture_ref[...]
+
+
 def on_device(tile_values, tile_row, tile_slot, tile_count, requests, right_side):
     n = lax.axis_size("rows")
     total, size, _ = tile_values.shape
@@ -348,11 +348,11 @@
     smem = pl.BlockSpec(memory_space=pltpu.SMEM)
     vmem = pl.BlockSpec(memory_space=pltpu.VMEM)
     dma = pltpu.SemaphoreType.DMA
-    return pl.pallas_call(
+    solved, picture = pl.pallas_call(
         functools.partial(kernel, n, chunk, 8),
         out_shape=(
             jax.ShapeDtypeStruct((blocks, systems, size), f32),
-            jax.ShapeDtypeStruct((systems, ITERS + 1, ITERS), f32),
+            jax.ShapeDtypeStruct((ITERS, systems, ITERS + 1), f32),
         ),
         in_specs=[pl.BlockSpec(memory_space=pl.ANY), vmem, vmem, smem, smem, vmem],
         out_specs=(vmem, vmem),
@@ -386,6 +386,17 @@
         requests.reshape(1, n),
         right_side,
     )
+    solved, picture = pl.pallas_call(
+        hand_on,
+        out_shape=(
+            jax.ShapeDtypeStruct(solved.shape, f32),
+            jax.ShapeDtypeStruct(picture.shape, f32),
+        ),
+        in_specs=[vmem, vmem],
+        out_specs=(vmem, vmem),
+        name="hand_on",
+    )(solved, picture)
+    return solved, jnp.transpose(picture, (1, 2, 0))
 
 
 def solution(mesh):

time: 44.9 us -> 43.4 us (0.967)
  local copies, waits for them, and re-layouts: 2.76 us -> 0 us
  Pallas kernels: 40.5 us -> 41.9 us
    pallas_call x1 -> x0, local copies, waits for them, and re-layouts: 1.39 us -> none  [on_device(): pl.pallas_call(functools.partial(kernel, n, chunk, 8), out_shape=(jax.Sha...]
    pallas_call x0 -> x1, Pallas kernels: none -> 1.38 us  [on_device(): pl.pallas_call(hand_on, out_shape=(jax.ShapeDtypeStruct(solved.shape, f32...]
    unnamed x1 -> x0, local copies, waits for them, and re-layouts: 1.37 us -> none
where the time goes in v3:
time: 43.4 us; the launch traced here: 43.2 us
  Pallas kernels  41.9 us (97%)
  between operations  1.28 us (3%)
    pallas_call x1, Pallas kernels, on_device(): pl.pallas_call(functools.partial(kernel, n, chunk, 8), out_shape=(jax.Sha...  40.5 us
    pallas_call x1, Pallas kernels, on_device(): pl.pallas_call(hand_on, out_shape=(jax.ShapeDtypeStruct(solved.shape, f32...  1.38 us

profile of v3, /device:TPU:0, one launch (start us, length us, event | category | flops | bytes accessed | tf_op | source)
XLA Modules:
  0.0 43.2 jit_solution(12440944111916769189)
XLA Ops:
  1.3 40.5 %cycle.1 = (f32[16,4,128]{2,1,0:T(4,128)}, f32[3,4,4]{2,1,0:T(4,128)}) custom-call(f32[112,128,128]{2,1,0:T(8,128)} %tile_hbm.1, s32[1,112]{1,0:T(1,128)} %bitcast.5, s32[1,1]{1,0:T(1,128)} %bitcast.4.count_ref, s32[112]{0:T(128)} %slot_ref.1, s32[1,32]{1,0:T(1,128)} %bitcast.6, f32[16,4,128]{2,1,0:T(4,128)} %right_ref.1), custom_call_target="tpu_custom_call" | custom-call | tf_op jit(solution)/shard_map/cycle/pallas_call | solution.py:351
  41.8 1.4 %hand_on.1 = (f32[16,4,128]{2,1,0:T(4,128)}, f32[3,4,4]{2,1,0:T(4,128)}) custom-call(f32[16,4,128]{2,1,0:T(4,128)} %get-tuple-element.6.solved_ref, f32[3,4,4]{2,1,0:T(4,128)} %get-tuple-element.7.picture_ref), custom_call_target="tpu_custom_call" | custom-call | tf_op jit(solution)/shard_map/hand_on/pallas_call | solution.py:389
